TPU v7x, 32 devices: a whole 2x2x4 slice. The times are simulated.
32 devices in a mesh: seq: 8 (over z, x), chan: 2 (over y), dp: 2 (over core).
Axes of the slice: x: 2, y: 2, z: 4, core: 2. Of those that a mesh axis runs over, the one named last changes fastest.
Arguments:
- ssm_input: bfloat16 [2, 1024, 4096], P('dp', 'seq', 'chan'), may hold values from -6 to 6
- gate_z: bfloat16 [2, 1024, 4096], P('dp', 'seq', 'chan'), may hold values from -6 to 6
- b_proj: bfloat16 [2, 1024, 128], P('dp', 'seq'), may hold values from -0.52734375 to 0.52734375
- c_proj: bfloat16 [2, 1024, 128], P('dp', 'seq'), may hold values from -6 to 6
- step_size: float32 [2, 1024, 64], P('dp', 'seq', 'chan'), may hold values from 0.02 to 0.2
- log_decay: float32 [2, 1024, 64], P('dp', 'seq', 'chan'), may hold values from -1 to 0, as said below
- skip_d: float32 [64], P('chan'), may hold values from 0.5 to 1.5
- norm_gain: float32 [4096], P('chan'), may hold values from 0.5 to 1.5
- w_out: bfloat16 [4096, 2048], P('chan'), may hold values from -0.09375 to 0.09375
- d_out: bfloat16 [2, 1024, 2048], P('dp', 'seq', 'chan'), may hold values from -6 to 6
- game_lengths: int32 [2, 4], P('dp'), may hold values from 1 to 512, 1024 in all within a row
Outputs:
- out: bfloat16 [2, 1024, 2048], P('dp', 'seq', 'chan')
- grad_x: bfloat16 [2, 1024, 4096], P('dp', 'seq', 'chan')
- grad_gain: float32 [4096], P('chan')
- grad_skip: float32 [64], P('chan')
Inputs may be any that keep to these rules, and one draw needn't show every extreme that they name: `game_lengths`: each row's 4 game lengths sum to 1024, and the longest is exactly 512. `log_decay`: a log decay per position and head.
All inputs are finite; a program needn't handle non-finite values.
Results may differ from a plain program's by a relative error of at most 0.017.
Values may be sent and summed in bfloat16 or wider, within the bound.
A program may use at most 64 MiB of HBM per device.

v0:
```python
import jax
import jax.numpy as jnp
from jax import lax
from jax.sharding import PartitionSpec as P

NORM_EPS = 1e-05
PRECISE = lax.Precision.HIGHEST


def prefix(value, axis, join, neutral):
    count = lax.axis_size(axis)
    place = lax.axis_index(axis)
    ahead = count - 1 - place
    gathered = jax.tree.map(
        lambda a, kind: lax.all_gather(a.astype(kind), axis), value, (jnp.bfloat16, jnp.bfloat16)
    )
    state = jax.tree.map(lambda a, e: jnp.zeros_like(a) + jnp.asarray(e, a.dtype), value, neutral)

    def one(hop, state):
        source = count - 1 - hop
        return join(
            state,
            jax.tree.map(
                lambda a, own: lax.dynamic_index_in_dim(a, source, 0, False).astype(own.dtype),
                gathered,
                value,
            ),
        )

    return lax.fori_loop(0, ahead, one, state)


def block_parts(c_block, b_block, dt_block, decay_block, reset_block):
    block_len = c_block.shape[0]
    running = jnp.cumsum(decay_block, axis=0)
    reset_count = jnp.cumsum(reset_block, axis=0)
    scores = lax.dot_general(
        c_block, b_block, (((1,), (1,)), ((), ())), preferred_element_type=jnp.float32
    )
    indices = jnp.arange(block_len, dtype=jnp.int32)
    allowed = (indices[:, None] >= indices[None, :]) & (
        reset_count[:, None] == reset_count[None, :]
    )
    log_gap = running.T[:, :, None] - running.T[:, None, :]
    mixing = (
        jnp.where(allowed[None], jnp.exp(jnp.minimum(log_gap, 0.0)), 0.0)
        * scores[None]
        * dt_block.T[:, None, :]
    )
    mixing = mixing.astype(jnp.bfloat16)
    end_count = reset_count[-1]
    carry_weight = jnp.where((reset_count == 0)[:, None], jnp.exp(running), 0.0)
    tail_weight = jnp.where(
        (reset_count == end_count)[:, None], jnp.exp(running[-1][None, :] - running), 0.0
    )
    block_decay = jnp.where(end_count == 0, jnp.exp(running[-1]), 0.0)
    return (mixing, carry_weight, tail_weight, block_decay)


def chain_link(earlier, later):
    return (earlier[0] * later[0], later[0][:, None, None] * earlier[1] + later[1])


def local(
    ssm_input,
    gate_z,
    b_proj,
    c_proj,
    step_size,
    log_decay,
    skip_d,
    norm_gain,
    w_out,
    d_out,
    game_lengths,
):
    seq_len = ssm_input.shape[1]
    local_width = ssm_input.shape[2]
    heads_here = step_size.shape[2]
    head_dim = local_width // heads_here
    state_dim = b_proj.shape[2]
    block_len = min(512, seq_len)
    count_blocks = seq_len // block_len
    total_width = local_width * lax.axis_size("chan")
    x_heads = ssm_input[0].reshape(seq_len, heads_here, head_dim)
    c_rows = c_proj[0]
    b_rows = b_proj[0]
    dt_rows = step_size[0]
    lengths = game_lengths[0]
    starts = jnp.cumsum(lengths) - lengths
    sequence_positions = lax.axis_index("seq") * seq_len + jnp.arange(seq_len, dtype=jnp.int32)
    resets = jnp.any(sequence_positions[:, None] == starts[None, :], axis=1).astype(jnp.int32)

    def blocked(array):
        return array.reshape((count_blocks, block_len) + array.shape[1:])

    zero_state = jnp.zeros((heads_here, state_dim, head_dim), jnp.float32)
    unit_decay = jnp.ones((heads_here,), jnp.float32)

    def forward_step(state_pair, block_inputs):
        local_state, before = state_pair
        x_block, c_block, b_block, dt_block, decay_block, reset_block = block_inputs
        mixing, carry_weight, tail_weight, block_decay = block_parts(
            c_block, b_block, dt_block, decay_block, reset_block
        )
        inside = jnp.einsum("hts,shp->thp", mixing, x_block, preferred_element_type=jnp.float32)
        carried = carry_weight[:, :, None] * jnp.einsum(
            "tn,hnp->thp", c_block.astype(jnp.float32), local_state, precision=PRECISE
        )
        scaled = ((tail_weight * dt_block)[:, :, None] * x_block).astype(jnp.bfloat16)
        fresh_state = jnp.einsum("sn,shp->hnp", b_block, scaled, preferred_element_type=jnp.float32)
        new_pair = (block_decay[:, None, None] * local_state + fresh_state, before * block_decay)
        return (
            new_pair,
            (
                inside + carried,
                carry_weight * before[None, :],
                mixing,
                carry_weight,
                tail_weight,
                block_decay,
            ),
        )

    forward_inputs = (
        blocked(x_heads),
        blocked(c_rows),
        blocked(b_rows),
        blocked(dt_rows),
        blocked(log_decay[0]),
        blocked(resets),
    )
    (dev_state, dev_decay), (
        ssd_blocks,
        incoming_weight,
        mixings,
        carry_weights,
        tail_weights,
        block_decays,
    ) = lax.scan(forward_step, (zero_state, unit_decay), forward_inputs)
    decays = lax.all_gather(dev_decay[None, :], "seq", axis=0, tiled=True)
    my_index = lax.axis_index("seq")
    device_ids = jnp.arange(decays.shape[0], dtype=jnp.int32)
    between = (device_ids[None, :] > device_ids[:, None]) & (device_ids[None, :] < my_index)
    weights = jnp.prod(jnp.where(between[:, :, None], decays[None, :, :], 1.0), axis=1)
    weights = weights * (device_ids < my_index).astype(jnp.float32)[:, None]
    incoming = zero_state + jnp.einsum(
        "mh,mhnp->hnp",
        weights,
        lax.all_gather(dev_state[None].astype(jnp.bfloat16), "seq", axis=0, tiled=True).astype(
            jnp.float32
        ),
        precision=PRECISE,
    )
    from_left = jnp.einsum("tn,hnp->thp", c_rows.astype(jnp.float32), incoming, precision=PRECISE)
    ssd_out = (
        ssd_blocks.reshape(seq_len, heads_here, head_dim)
        + incoming_weight.reshape(seq_len, heads_here)[:, :, None] * from_left
    )
    ssd_out = ssd_out + skip_d[None, :, None] * x_heads.astype(jnp.float32)
    gate_act = jax.nn.silu(gate_z[0].astype(jnp.float32))
    gated = ssd_out.reshape(seq_len, local_width) * gate_act
    square_total = lax.psum(jnp.sum(gated * gated, axis=1), "chan")
    inv_rms = lax.rsqrt(square_total / total_width + NORM_EPS)
    normed = (gated * norm_gain).astype(jnp.bfloat16)
    w_cols = w_out
    projected = (
        lax.psum_scatter(
            lax.dot_general(
                w_cols, normed, (((0,), (1,)), ((), ())), preferred_element_type=jnp.float32
            ).astype(jnp.bfloat16),
            "chan",
            scatter_dimension=0,
            tiled=True,
        )
        .astype(jnp.float32)
        .T
    )
    out = (inv_rms[:, None] * projected).astype(jnp.bfloat16)[None]
    cotangent = d_out[0]
    w_cols = w_out
    pulled = lax.dot_general(
        lax.all_gather(cotangent, "chan", axis=1, tiled=True),
        w_cols,
        (((1,), (1,)), ((), ())),
        preferred_element_type=jnp.float32,
    )
    out_dot = lax.psum(jnp.sum(normed.astype(jnp.float32) * pulled, axis=1), "chan")
    d_normed = inv_rms[:, None] * pulled
    gain_local = jnp.sum(gated * d_normed, axis=0)
    d_ssd = (
        (norm_gain * d_normed - (inv_rms**3 * out_dot / total_width)[:, None] * gated) * gate_act
    ).astype(jnp.bfloat16)
    d_heads = d_ssd.reshape(seq_len, heads_here, head_dim)
    skip_local = jnp.sum(d_heads.astype(jnp.float32) * x_heads.astype(jnp.float32), axis=(0, 2))
    grad_gain, grad_skip = lax.psum((gain_local, skip_local), ("seq", "dp"))

    def backward_step(state_pair, block_inputs):
        local_adjoint, later_decay = state_pair
        d_block, c_block, b_block, dt_block, mixing, carry_weight, tail_weight, block_decay = (
            block_inputs
        )
        inside = jnp.einsum("hts,thp->shp", mixing, d_block, preferred_element_type=jnp.float32)
        carried = (dt_block * tail_weight)[:, :, None] * jnp.einsum(
            "sn,hnp->shp", b_block.astype(jnp.float32), local_adjoint, precision=PRECISE
        )
        weighted = (carry_weight[:, :, None] * d_block).astype(jnp.bfloat16)
        fresh_adjoint = jnp.einsum(
            "tn,thp->hnp", c_block, weighted, preferred_element_type=jnp.float32
        )
        new_pair = (
            fresh_adjoint + block_decay[:, None, None] * local_adjoint,
            later_decay * block_decay,
        )
        return (new_pair, (inside + carried, dt_block * tail_weight * later_decay[None, :]))

    backward_inputs = (
        blocked(d_heads),
        blocked(c_rows),
        blocked(b_rows),
        blocked(dt_rows),
        mixings,
        carry_weights,
        tail_weights,
        block_decays,
    )
    (dev_adjoint, _), (grad_blocks, outgoing_weight) = lax.scan(
        backward_step, (zero_state, unit_decay), backward_inputs, reverse=True
    )
    _, from_right = prefix((dev_decay, dev_adjoint), "seq", chain_link, (unit_decay, zero_state))
    right_terms = jnp.einsum(
        "sn,hnp->shp", b_rows.astype(jnp.float32), from_right, precision=PRECISE
    )
    grad_heads = (
        grad_blocks.reshape(seq_len, heads_here, head_dim)
        + outgoing_weight.reshape(seq_len, heads_here)[:, :, None] * right_terms
    )
    grad_heads = grad_heads + skip_d[None, :, None] * d_heads.astype(jnp.float32)
    grad_x = grad_heads.astype(jnp.bfloat16).reshape(1, seq_len, local_width)
    return (out, grad_x, grad_gain, grad_skip)


def solution(mesh):
    return jax.shard_map(
        local,
        mesh=mesh,
        in_specs=(
            P("dp", "seq", "chan"),
            P("dp", "seq", "chan"),
            P("dp", "seq", None),
            P("dp", "seq", None),
            P("dp", "seq", "chan"),
            P("dp", "seq", "chan"),
            P("chan"),
            P("chan"),
            P("chan", None),
            P("dp", "seq", "chan"),
            P("dp", None),
        ),
        out_specs=(P("dp", "seq", "chan"), P("dp", "seq", "chan"), P("chan"), P("chan")),
        check_vma=False,
    )
```

profile of v0, /device:TPU:0, one launch (start us, length us, event | category | flops | bytes accessed | tf_op | source)
XLA Modules:
  0.0 248.1 jit_solution(2390316497509367646)
XLA Ops:
  18.2 22.6 %all-gather.3 = f32[8,1,32]{2,1,0:T(1,128)S(1)} all-gather(f32[1,1,32]{2,1,0:T(1,128)S(1)} %get-tuple-element.227), channel_id=1, replica_groups=mesh['seq'=8,'chan'=2,'dp'=2] {'seq'}, dimensions={0}, use_global_device_ids=true | all-gather | bytes 1152 | tf_op jit(solution)/shard_map/all_gather | solution.py:141
  40.9 7.1 %all-gather.1 = bf16[1,128,2048]{2,1,0:T(8,128)(2,1)} all-gather(bf16[1,128,1024]{2,1,0:T(8,128)(2,1)S(1)} %copy-done.7), channel_id=3, replica_groups=mesh['seq'=8,'chan'=2,'dp'=2] {'chan'}, dimensions={2}, use_global_device_ids=true | all-gather | bytes 786432 | tf_op jit(solution)/shard_map/all_gather | solution.py:183
  48.4 2.1 convolution_bitcast_fusion.5
  51.1 40.1 %all-gather.8.cloned.1.call-done = bf16[256,128,64]{1,2,0:T(8,128)(2,1)} async-done(((bf16[32,128,64]{1,2,0:T(8,128)(2,1)}), bf16[256,128,64]{1,2,0:T(8,128)(2,1)}) %all-gather.8.cloned.1.call-update) | async-done | bytes 4194320 | tf_op jit(solution)/shard_map/all_gather | solution.py:150
  91.1 3.2 %multiply_reduce_fusion = f32[32,128,64]{1,2,0:T(8,128)S(1)} fusion(bf16[32,8,128,64]{2,3,0,1:T(8,128)(2,1)} %bitcast.158, f32[32,8]{0,1:T(8,128)S(1)} %multiply_bitcast_fusion), kind=kLoop, calls=%fused_computation.3 | loop fusion | flops 6029312 | bytes 5243904 | tf_op jit(solution)/shard_map/mh,mhnp->hnp/dot_general | solution.py:147
  94.4 1.9 multiply_reduce_fusion.3
  96.3 1.6 copy.91
  97.9 4.9 %psum.28 = f32[128]{0:T(128)S(1)} all-reduce(f32[128]{0:T(128)S(1)} %get-tuple-element.232), channel_id=1, replica_groups=mesh['seq'=8,'chan'=2,'dp'=2] {'chan'}, use_global_device_ids=true, to_apply=%region_6.7 | all-reduce | flops 128 | bytes 1024 | tf_op jit(solution)/shard_map/psum | solution.py:163
  102.9 5.6 %fusion = bf16[2048,128]{0,1:T(8,128)(2,1)} fusion(bf16[2048,2048]{1,0:T(8,128)(2,1)} %param.21, f32[2048]{0:T(1024)S(1)} %copy-done.9, f32[128,2048]{1,0:T(8,128)S(1)} %copy.91, bf16[1,128,2048]{2,1,0:T(8,128)(2,1)S(1)} %copy-done.3), kind=kOutput, calls=%fused_computation.5 | convolution fusion | flops 1076101120 | bytes 10493952 | tf_op jit(solution)/shard_map/dot_general | solution.py:169
  108.4 7.6 %multiply_reduce_fusion.1 = (f32[2048]{0:T(1024)S(1)}, f32[128]{0:T(128)S(1)}, f32[128,2048]{1,0:T(8,128)}) fusion(f32[128]{0:T(128)S(1)} %add_rsqrt_fusion, f32[128,2048]{1,0:T(8,128)S(1)} %copy.91, bf16[1,128,2048]{2,1,0:T(8,128)(2,1)S(1)} %copy-done.3, f32[2048]{0:T(1024)S(1)} %copy-done.9, bf16[2048,2048]{1,0:T(8,128)(2,1)} %param.21, ...), kind=kOutput, calls=%fused_computation.42 | convolution fusion | flops 1077409664 | bytes 11551744 | tf_op jit(solution)/shard_map/dot_general | solution.py:182
  116.0 4.9 %psum.29 = f32[128]{0:T(128)S(1)} all-reduce(f32[128]{0:T(128)S(1)} %get-tuple-element.210), channel_id=1, replica_groups=mesh['seq'=8,'chan'=2,'dp'=2] {'chan'}, use_global_device_ids=true, to_apply=%region_9.10 | all-reduce | flops 128 | bytes 1024 | tf_op jit(solution)/shard_map/psum | solution.py:188
  121.0 2.1 fusion.18
  124.6 18.1 %all-gather.4 = bf16[8,1,32]{2,1,0:T(2,128)(2,1)S(1)} all-gather(bf16[1,1,32]{2,1,0:T(2,128)(2,1)S(1)} %get-tuple-element.225), channel_id=1, replica_groups=mesh['seq'=8,'chan'=2,'dp'=2] {'seq'}, dimensions={0}, use_global_device_ids=true | all-gather | bytes 576 | tf_op jit(solution)/shard_map/all_gather | solution.py:15
  143.2 33.1 %all-reduce = (f32[2048]{0:T(1024)}, f32[32]{0:T(128)}) all-reduce(f32[2048]{0:T(1024)S(1)} %get-tuple-element.209, f32[32]{0:T(128)S(1)} %reduce_sum.48), channel_id=1, replica_groups=mesh['seq'=8,'chan'=2,'dp'=2] {'seq','dp'}, use_global_device_ids=true, to_apply=%region_13.14 | all-reduce | flops 2080 | bytes 16640 | tf_op jit(solution)/shard_map/psum | solution.py:196
  177.0 1.6 fusion.4
  178.6 1.8 fusion.26
  180.4 29.6 %all-gather.10.cloned.1.call-done = bf16[256,128,64]{1,2,0:T(8,128)(2,1)} async-done(((bf16[32,128,64]{1,2,0:T(8,128)(2,1)}), bf16[256,128,64]{1,2,0:T(8,128)(2,1)}) %all-gather.10.cloned.1.call-update) | async-done | bytes 4194320 | tf_op jit(solution)/shard_map/all_gather | solution.py:15
  210.2 27.1 %while.9 = (s32[]{:T(128)}, f32[32,128,64]{2,1,0:T(8,128)S(1)}, s32[]{:T(128)}, bf16[8,32]{1,0:T(8,128)(2,1)S(1)}, bf16[8,32,128,64]{2,3,1,0:T(8,128)(2,1)}, /*index=5*/s32[]{:T(128)}, s32[]{:T(128)}, s32[]{:T(128)}, s32[]{:T(128)}) while((s32[]{:T(128)}, f32[32,128,64]{2,1,0:T(8,128)S(1)}, s32[]{:T(128)}, bf16[8,32]{1,0:T(8,128)(2,1)S(1)}, ...), condition=%wide.region_11.12_spmd, body=%wide.region_10.11_spmd.sunk | while | flops 786470 | bytes 4719059 | solution.py:30
  210.2 1.9 constant_dynamic-slice_fusion.2
  212.1 1.5 copy.114
  214.1 1.9 constant_dynamic-slice_fusion.2
  215.9 1.5 copy.114
  217.9 1.9 constant_dynamic-slice_fusion.2
  219.8 1.5 copy.114
  221.8 1.9 constant_dynamic-slice_fusion.2
  223.7 1.5 copy.114
  225.7 1.9 constant_dynamic-slice_fusion.2
  227.5 1.5 copy.114
  229.5 1.9 constant_dynamic-slice_fusion.2
  233.4 1.9 constant_dynamic-slice_fusion.2
  235.3 1.5 copy.114
  237.3 3.2 %fusion.13 = bf16[128,32,64]{0,2,1:T(8,128)(2,1)S(1)} fusion(f32[128,32,64]{0,2,1:T(8,128)} %fusion.4, f32[32,128,64]{2,1,0:T(8,128)S(1)} %get-tuple-element.172, bf16[128,32,64]{0,2,1:T(8,128)(2,1)} %bitcast.162, f32[32]{0:T(128)S(1)} %copy-done.10, f32[128,32]{0,1:T(8,128)S(1)} %copy.87, bf16[1,128,128]{2,1,0:T(8,128)(2,1)S(1)} %copy-done.5), kind=kOutput, calls=%fused_computation.31 | convolution fusion | flops 404226048 | bytes 3195008 | tf_op jit(solution)/shard_map/sn,hnp->shp/dot_general | solution.py:231
  (92 shorter events, 19.9 us)
Async XLA Ops:
  7.2 41.1 %copy-start = (bf16[1,128,128]{2,1,0:T(8,128)(2,1)S(1)}, bf16[1,128,128]{2,1,0:T(8,128)(2,1)}, u32[]{:S(2)}) copy-start(bf16[1,128,128]{2,1,0:T(8,128)(2,1)} %param.16) | copy-start | bytes 98308
  7.2 6.4 %copy-start.1 = (bf16[1,128,2048]{2,1,0:T(8,128)(2,1)S(1)}, bf16[1,128,2048]{2,1,0:T(8,128)(2,1)}, u32[]{:S(2)}) copy-start(bf16[1,128,2048]{2,1,0:T(8,128)(2,1)} %param.13) | copy-start | bytes 1572868
  7.2 84.0 %all-gather.8.cloned.1.call-start = ((), (), s32[]{:S(2)}) async-start(), calls=%async_computation.2 | async-start | bytes 4718592 | tf_op jit(solution)/shard_map/all_gather | solution.py:150
  13.6 0.8 copy-start.5
  13.7 2.9 %copy-start.3 = (bf16[1,128,2048]{2,1,0:T(8,128)(2,1)S(1)}, bf16[1,128,2048]{2,1,0:T(8,128)(2,1)}, u32[]{:S(2)}) copy-start(bf16[1,128,2048]{2,1,0:T(8,128)(2,1)} %param.14) | copy-start | bytes 1572868
  15.4 163.2 %reduce-scatter.2.cloned.1.call-start = ((), (), s32[]{:S(2)}) async-start(), calls=%async_computation.1 | async-start | bytes 786432 | tf_op jit(solution)/shard_map/reduce_scatter | solution.py:168
  16.6 24.3 %copy-start.7 = (bf16[1,128,1024]{2,1,0:T(8,128)(2,1)S(1)}, bf16[1,128,1024]{2,1,0:T(8,128)(2,1)}, u32[]{:S(2)}) copy-start(bf16[1,128,1024]{2,1,0:T(8,128)(2,1)} %param.22) | copy-start | bytes 786436
  17.8 30.6 %copy-start.8 = (f32[1,128,32]{1,2,0:T(8,128)S(1)}, f32[1,128,32]{1,2,0:T(8,128)}, u32[]{:S(2)}) copy-start(f32[1,128,32]{1,2,0:T(8,128)} %param.17) | copy-start | bytes 49156
  91.1 3.3 %copy-start.4 = (f32[1,128,2048]{1,2,0:T(8,128)S(1)}, f32[1,128,2048]{1,2,0:T(8,128)}, u32[]{:S(2)}) copy-start(f32[1,128,2048]{1,2,0:T(8,128)} %copy.90) | copy-start | bytes 3145732
  91.1 3.3 %copy-start.6 = (bf16[1,128,2048]{1,2,0:T(8,128)(2,1)S(1)}, bf16[1,128,2048]{1,2,0:T(8,128)(2,1)}, u32[]{:S(2)}) copy-start(bf16[1,128,2048]{1,2,0:T(8,128)(2,1)} %copy.84) | copy-start | bytes 1572868
  91.1 3.3 %copy-start.10 = (f32[32]{0:T(128)S(1)}, f32[32]{0:T(128)}, u32[]{:S(2)}) copy-start(f32[32]{0:T(128)} %param.19) | copy-start | bytes 388
  96.3 6.5 %copy-start.9 = (f32[2048]{0:T(1024)S(1)}, f32[2048]{0:T(1024)}, u32[]{:S(2)}) copy-start(f32[2048]{0:T(1024)} %param.20) | copy-start | bytes 24580
  121.0 89.0 %all-gather.10.cloned.1.call-start = ((), (), s32[]{:S(2)}) async-start(), calls=%async_computation.3 | async-start | bytes 4718592 | tf_op jit(solution)/shard_map/all_gather | solution.py:15
  143.0 67.0 %copy-start.2 = (bf16[128,2048]{0,1:T(8,128)(2,1)}, bf16[128,2048]{0,1:T(8,128)(2,1)S(1)}, u32[]{:S(2)}) copy-start(bf16[128,2048]{0,1:T(8,128)(2,1)S(1)} %copy.92) | copy-start | bytes 1572868
Sparse Core Ops, SparseCore 0:
  15.6 75.5 all-gather.7
  121.1 13.1 reduce-scatter.1
  136.4 73.4 all-gather.9
where the time goes:
time: 249 us; the launch traced here: 248 us
  blocking collectives  90.7 us (36%)
  waiting for transfers between devices  69.7 us (28%)
  local copies, waits for them, and re-layouts  33.3 us (13%)
  matrix products  25.7 us (10%)
  between operations  14.7 us (6%)
  other arithmetic  13.6 us (5%)
    all_gather x1, waiting for transfers between devices, local(): lax.all_gather(dev_state[None].astype(jnp.bfloat16), 'seq', axis=0, tiled...  40.1 us
    psum x1, blocking collectives, local(): grad_gain, grad_skip = lax.psum((gain_local, skip_local), ('seq', 'dp'))  33.1 us
    all_gather x1, waiting for transfers between devices, prefix(): lax.all_gather(a.astype(kind), axis)  29.6 us
    dynamic_slice x14, local copies, waits for them, and re-layouts, one(): lax.dynamic_index_in_dim(a, source, 0, False).astype(own.dtype)  23.7 us
    all_gather x1, blocking collectives, local(): decays = lax.all_gather(dev_decay[None, :], 'seq', axis=0, tiled=True)  22.6 us
    all_gather x1, blocking collectives, prefix(): lax.all_gather(a.astype(kind), axis)  18.1 us
    dot_general x1, matrix products, local(): lax.dot_general(lax.all_gather(cotangent, 'chan', axis=1, tiled=True), w_...  7.57 us
    all_gather x1, blocking collectives, local(): lax.all_gather(cotangent, 'chan', axis=1, tiled=True)  7.15 us
  transfers between devices with their start and end apart: 3, of which 2 were waited for; matrix products, arithmetic and copies ran while one was open for 6% of the time, Pallas kernels for 0%

commit v1 on v0

v1 whole, which is shorter than its diff:
```python
import functools

import jax
import jax.numpy as jnp
from jax import lax
from jax.experimental import pallas as pl
from jax.experimental.pallas import tpu as pltpu
from jax.sharding import PartitionSpec as P

NORM_EPS = 1e-05
F32 = jnp.float32
BF16 = jnp.bfloat16
MESH = pl.DeviceIdType.MESH
FWD, BWD = 0, 1


def dot(a, b):
    return lax.dot_general(a, b, (((1,), (0,)), ((), ())), preferred_element_type=F32)


def dot_rows(a, b):
    return lax.dot_general(a, b, (((0,), (0,)), ((), ())), preferred_element_type=F32)


def dot_cols(a, b):
    return lax.dot_general(a, b, (((1,), (1,)), ((), ())), preferred_element_type=F32)


def split(value, terms):
    parts = []
    for _ in range(terms):
        part = value.astype(BF16)
        parts.append(part)
        value = value - part.astype(F32)
    return parts


def kernel(
    sizes,
    x_ref,
    b_ref,
    c_ref,
    dt_ref,
    ld_ref,
    skip_ref,
    gain_ref,
    gl_ref,
    z_hbm,
    w_hbm,
    do_hbm,
    out_ref,
    gx_ref,
    gg_ref,
    gs_ref,
    z_ref,
    w_ref,
    dfull,
    running_ref,
    run_row,
    decay_row,
    decay_peer,
    carry_e,
    tdt_e,
    mix_ref,
    inside_ref,
    act_ref,
    gated_ref,
    normed_ref,
    pulled_ref,
    d_ref,
    own_ref,
    tx1,
    rx1,
    txc,
    rxc,
    tx3,
    state_ref,
    stat_tx,
    stat_rx,
    proj_tx,
    proj_rx,
    red_tx,
    red_rx,
    load_sem,
    dl_sem,
    do_send,
    do_recv,
    dec_sem,
    s1_send,
    s1_recv,
    sc_send,
    sc_recv,
    s3_send,
    s3_recv,
    st_send,
    st_recv,
    pj_send,
    pj_recv,
    rd_send,
    rd_recv,
):
    n_seq, n_chan, n_dp, heads, games, chunks = sizes
    rows, width = x_ref.shape
    hd = width // heads
    half = width // 2
    cw = half // chunks
    total_width = width * n_chan
    nb = out_ref.shape[1]
    seq = lax.axis_index("seq")
    chan = lax.axis_index("chan")
    dp = lax.axis_index("dp")
    mine = lax.rem(seq, 2)
    partner = {"seq": seq + 1 - 2 * mine}
    place = seq // 2
    last = n_seq // 2 - 1

    steps = []
    hop = 1
    while hop < n_seq:
        steps.append({"seq": seq + hop - 2 * hop * lax.rem(seq // hop, 2)})
        hop *= 2
    hop = 1
    while hop < n_dp:
        steps.append({"dp": dp + hop - 2 * hop * lax.rem(dp // hop, 2)})
        hop *= 2
    chan_peers = [{"chan": lax.rem(chan + off, n_chan)} for off in range(1, n_chan)]
    greet = steps + chan_peers + [
        {"seq": lax.rem(seq + 2, n_seq)},
        {"seq": lax.rem(seq + n_seq - 2, n_seq)},
    ]
    barrier = pltpu.get_barrier_semaphore()
    for peer in greet:
        pl.semaphore_signal(barrier, inc=1, device_id=peer, device_id_type=MESH)

    loads = [
        pltpu.make_async_copy(z_hbm, z_ref, load_sem.at[0]),
        pltpu.make_async_copy(w_hbm, w_ref, load_sem.at[1]),
        pltpu.make_async_copy(do_hbm, dfull.at[0], dl_sem),
    ]
    loads[2].start()
    loads[0].start()
    loads[1].start()

    def remote(src, dst, ssem, rsem, peer):
        return pltpu.make_async_remote_copy(
            src_ref=src, dst_ref=dst, send_sem=ssem, recv_sem=rsem, device_id=peer, device_id_type=MESH
        )

    row_i = lax.broadcasted_iota(jnp.int32, (rows, rows), 0)
    col_i = lax.broadcasted_iota(jnp.int32, (rows, rows), 1)
    causal = row_i >= col_i
    tri = causal.astype(F32).astype(BF16)
    running = jnp.zeros((rows, heads), F32)
    for part in split(ld_ref[...], 3):
        running = running + dot(tri, part)
    running_ref[...] = running
    run_row[...] = running.T
    base = seq * rows
    count_col = jnp.zeros((rows, 1), jnp.int32)
    count_row = jnp.zeros((1, rows), jnp.int32)
    count_end = jnp.zeros((1, 1), jnp.int32)
    pos_col = base + lax.broadcasted_iota(jnp.int32, (rows, 1), 0)
    pos_row = base + lax.broadcasted_iota(jnp.int32, (1, rows), 1)
    pos_end = base + rows - 1 + lax.broadcasted_iota(jnp.int32, (1, 1), 0)
    begin = jnp.int32(0)
    for g in range(games):
        from_here = (begin >= base).astype(jnp.int32)
        count_col = count_col + (pos_col >= begin).astype(jnp.int32) * from_here
        count_row = count_row + (pos_row >= begin).astype(jnp.int32) * from_here
        count_end = count_end + (pos_end >= begin).astype(jnp.int32) * from_here
        begin = begin + gl_ref[0, g]
    end = running[rows - 1 : rows, :]
    carry = jnp.where(count_col == 0, jnp.exp(running), 0.0)
    tail = jnp.where(count_col == count_end, jnp.exp(end - running), 0.0)
    decay = jnp.where(count_end == 0, jnp.exp(end), 0.0)
    spread = (
        lax.broadcasted_iota(jnp.int32, (heads, width), 1) // hd
        == lax.broadcasted_iota(jnp.int32, (heads, width), 0)
    ).astype(F32).astype(BF16)

    def expand(value, terms):
        total = None
        for part in split(value, terms):
            piece = dot(part, spread)
            total = piece if total is None else total + piece
        return total

    tdt_e[...] = expand(tail * dt_ref[...], 2)
    row_pad = jnp.concatenate([decay, skip_ref[...], jnp.zeros((6, heads), F32)], axis=0)
    rows_e = expand(row_pad, 3)
    decay_row[...] = rows_e[0:1, :]
    skip_e = rows_e[1:2, :]

    def other_cols(c):
        return pl.ds(pl.multiple_of((1 - mine) * half + c * cw, cw), cw)

    def my_cols(c):
        return pl.ds(pl.multiple_of(mine * half + c * cw, cw), cw)

    def send1(d, c):
        return remote(tx1.at[d, c], rx1.at[d, c], s1_send.at[d, c], s1_recv.at[d, c], partner)

    def send3(d, c):
        return remote(
            tx3.at[d, c], state_ref.at[d, mine * chunks + c], s3_send.at[d, c], s3_recv.at[d, c], partner
        )

    def sendc(d, c):
        to = lax.rem(seq + (2 if d == FWD else n_seq - 2), n_seq)
        return remote(txc.at[d, c], rxc.at[d, c], sc_send.at[d, c], sc_recv.at[d, c], {"seq": to})

    has = (place > 0, place < last)
    dec = remote(decay_row, decay_peer, dec_sem.at[0], dec_sem.at[1], partner)

    def make(d, left, value_of):
        for c in range(chunks):
            tx1[d, c] = dot(left, value_of(other_cols(c))).astype(BF16)
            send1(d, c).start()
        for c in range(chunks):
            own_ref[c] = dot(left, value_of(my_cols(c)))

    def chain(d):
        first = mine == (0 if d == FWD else 1)
        prev, nxt = (has[0], has[1]) if d == FWD else (has[1], has[0])

        def body(c, _):
            send1(d, c).wait_recv()

            @pl.when(prev)
            def _():
                sendc(d, c).wait_recv()

            @pl.when(jnp.logical_not(prev))
            def _():
                rxc[d, c] = jnp.zeros((rxc.shape[2], cw), BF16)

            dec_me = decay_row[:, my_cols(c)]
            dec_peer = decay_peer[:, my_cols(c)]
            fresh = own_ref[c]
            fresh_peer = rx1[d, c].astype(F32)
            before = rxc[d, c].astype(F32)
            after_me = dec_me * before + fresh
            after_peer = dec_peer * before + fresh_peer

            @pl.when(nxt)
            def _():
                txc[d, c] = jnp.where(
                    first, dec_peer * after_me + fresh_peer, dec_me * after_peer + fresh
                ).astype(BF16)
                sendc(d, c).start()

            tx3[d, c] = jnp.where(first, after_me, before).astype(BF16)
            send3(d, c).start()
            state_ref[d, mine * chunks + c] = jnp.where(first, before, after_peer).astype(BF16)
            return 0

        lax.fori_loop(0, chunks, body, 0)

    pl.semaphore_wait(barrier, len(greet))
    dec.start()
    b_t = b_ref[...].T
    make(FWD, b_t, lambda cols: (tdt_e[:, cols] * x_ref[:, cols].astype(F32)).astype(BF16))
    loads[2].wait()
    do_copies = []
    for k, peer in enumerate(chan_peers):
        do_copies.append(remote(dfull.at[0], dfull.at[k + 1], do_send.at[k], do_recv.at[k], peer))
        do_copies[-1].start()

    scores = jnp.where(causal & (count_col == count_row), dot_cols(c_ref[...], b_ref[...]), 0.0)
    dt_row = dt_ref[...].T
    pos_lane = lax.broadcasted_iota(jnp.int32, (rows, 2 * hd), 1) < hd
    carry_e[...] = expand(carry, 2)
    loads[0].wait()

    def block_diag(pair):
        pair = pair.astype(F32)
        return jnp.concatenate(
            [jnp.where(pos_lane, pair, 0.0), jnp.where(pos_lane, 0.0, pair)], axis=0
        ).astype(BF16)

    for q in range(heads // 2):
        cols = slice(q * 2 * hd, (q + 1) * 2 * hd)
        mixes = []
        for h in (2 * q, 2 * q + 1):
            gap = jnp.minimum(running_ref[:, h : h + 1] - run_row[h : h + 1, :], 0.0)
            mixes.append((jnp.exp(gap) * scores * dt_row[h : h + 1, :]).astype(BF16))
            mix_ref[q, (h % 2) * rows : (h % 2 + 1) * rows, :] = mixes[-1]
        pair = x_ref[:, cols]
        inside_ref[:, cols] = dot(jnp.concatenate(mixes, axis=1), block_diag(pair)) + skip_e[
            :, cols
        ] * pair.astype(F32)
        zf = z_ref[:, cols].astype(F32)
        act_ref[:, cols] = zf / (1.0 + jnp.exp(-zf))

    dec.wait_recv()
    chain(FWD)

    loads[1].wait()
    for copy in do_copies:
        copy.wait_recv()
    tile = min(256, width)

    def pull(i, _):
        feats = pl.ds(pl.multiple_of(i * tile, tile), tile)
        total = None
        for k in range(n_chan):
            source = lax.rem(chan + n_chan - k, n_chan)
            piece = dot_cols(dfull[k], w_ref[feats, pl.ds(pl.multiple_of(source * nb, nb), nb)])
            total = piece if total is None else total + piece
        pulled_ref[:, feats] = total
        return 0

    lax.fori_loop(0, width // tile, pull, 0)

    def gate(q, sums):
        squares, dots = sums
        cols = pl.ds(pl.multiple_of(q * cw, cw), cw)
        carried = dot(c_ref[...], state_ref[FWD, q])
        gated = (inside_ref[:, cols] + carry_e[:, cols] * carried) * act_ref[:, cols]
        normed = (gated * gain_ref[:, cols]).astype(BF16)
        gated_ref[:, cols] = gated
        normed_ref[:, cols] = normed
        sq = gated * gated
        od = normed.astype(F32) * pulled_ref[:, cols]
        for k in range(cw // 128):
            squares = squares + sq[:, k * 128 : (k + 1) * 128]
            dots = dots + od[:, k * 128 : (k + 1) * 128]
        return squares, dots

    zero = jnp.zeros((rows, 128), F32)
    sums = lax.fori_loop(0, chunks, lambda c, s: gate(mine * chunks + c, s), (zero, zero))

    def gate_late(d):
        def body(c, s):
            send3(d, c).wait_recv()
            return gate((1 - mine) * chunks + c, s)

        return body

    squares, dots = lax.fori_loop(0, chunks, gate_late(FWD), sums)
    sq_col = jnp.sum(squares, axis=1, keepdims=True)
    dot_col = jnp.sum(dots, axis=1, keepdims=True)
    lane = lax.broadcasted_iota(jnp.int32, (rows, 128), 1)
    stats = jnp.where(lane == 0, sq_col, jnp.where(lane == 1, dot_col, 0.0))
    stat_tx[...] = stats.T[0:8, :]
    st_copies = []
    for k, peer in enumerate(chan_peers):
        st_copies.append(remote(stat_tx, stat_rx.at[k], st_send.at[k], st_recv.at[k], peer))
        st_copies[-1].start()
    total = stat_tx[...]
    for k, copy in enumerate(st_copies):
        copy.wait_recv()
        total = total + stat_rx[k]
    stat_cols = jnp.concatenate([total, jnp.zeros((rows - 8, rows), F32)], axis=0).T
    inv = lax.rsqrt(stat_cols[:, 0:1] / total_width + NORM_EPS)
    back = inv * inv * inv * stat_cols[:, 1:2] / total_width

    def cot(q, _):
        cols = pl.ds(pl.multiple_of(q * cw, cw), cw)
        gated = gated_ref[:, cols]
        d_normed = inv * pulled_ref[:, cols]
        d = ((gain_ref[:, cols] * d_normed - back * gated) * act_ref[:, cols]).astype(BF16)
        d_ref[:, cols] = d
        red_tx[0, 0:1, cols] = jnp.sum(gated * d_normed, axis=0, keepdims=True)
        red_tx[0, 1:2, cols] = jnp.sum(
            d.astype(F32) * x_ref[:, cols].astype(F32), axis=0, keepdims=True
        )
        return 0

    lax.fori_loop(0, 2 * chunks, cot, 0)
    c_t = c_ref[...].T
    make(BWD, c_t, lambda cols: (carry_e[:, cols] * d_ref[:, cols].astype(F32)).astype(BF16))

    def red(k):
        return remote(red_tx.at[k], red_rx.at[k], rd_send.at[k], rd_recv.at[k], steps[k])

    def reduce_step(k):
        red(k).wait_recv()
        red_tx[k + 1] = red_tx[k] + red_rx[k]
        if k + 1 < len(steps):
            red(k + 1).start()

    red(0).start()

    tile_n = min(256, nb)

    def project(block, store):
        def body(i, _):
            at = pl.ds(pl.multiple_of(block * nb + i * tile_n, tile_n), tile_n)
            store(pl.ds(pl.multiple_of(i * tile_n, tile_n), tile_n), dot(normed_ref[...], w_ref[:, at]))
            return 0

        lax.fori_loop(0, nb // tile_n, body, 0)

    pj_copies = []
    for k, peer in enumerate(chan_peers):

        def store(at, value, k=k):
            proj_tx[k, :, at] = value.astype(BF16)

        project(peer["chan"], store)
        pj_copies.append(remote(proj_tx.at[k], proj_rx.at[k], pj_send.at[k], pj_recv.at[k], peer))
        pj_copies[-1].start()

    chain(BWD)
    reduce_step(0)

    own_tiles = []
    for i in range(nb // tile_n):
        at = pl.ds(pl.multiple_of(chan * nb + i * tile_n, tile_n), tile_n)
        own_tiles.append(dot(normed_ref[...], w_ref[:, at]))
    for copy in pj_copies:
        copy.wait_recv()
    for i in range(nb // tile_n):
        at = slice(i * tile_n, (i + 1) * tile_n)
        value = own_tiles[i]
        for k in range(n_chan - 1):
            value = value + proj_rx[k, :, at].astype(F32)
        out_ref[:, at] = (inv * value).astype(BF16)
    if len(steps) > 1:
        reduce_step(1)

    for q in range(heads // 2):
        cols = slice(q * 2 * hd, (q + 1) * 2 * hd)
        pair = d_ref[:, cols]
        inside_ref[:, cols] = dot_rows(mix_ref[q], block_diag(pair)) + skip_e[:, cols] * pair.astype(F32)
    for k in range(2, len(steps)):
        reduce_step(k)

    def finish(q):
        cols = pl.ds(pl.multiple_of(q * cw, cw), cw)
        carried = dot(b_ref[...], state_ref[BWD, q])
        gx_ref[:, cols] = (inside_ref[:, cols] + tdt_e[:, cols] * carried).astype(BF16)

    def early(c, _):
        finish(mine * chunks + c)
        return 0

    def late(c, _):
        send3(BWD, c).wait_recv()
        finish((1 - mine) * chunks + c)
        return 0

    lax.fori_loop(0, chunks, early, 0)
    lax.fori_loop(0, chunks, late, 0)

    final = red_tx[len(steps)]
    gg_ref[...] = final[0:1, :]
    skip_cols = jnp.concatenate([final[1:2, :], jnp.zeros((7, width), F32)], axis=0)
    skip_sum = jnp.zeros((8, heads), F32)
    for part in split(skip_cols, 3):
        skip_sum = skip_sum + dot_cols(part, spread)
    gs_ref[...] = skip_sum[0:1, :]

    dec.wait_send()
    for copy in do_copies + st_copies + pj_copies:
        copy.wait_send()
    for k in range(len(steps)):
        red(k).wait_send()
    for d in (FWD, BWD):
        for c in range(chunks):
            send1(d, c).wait_send()
            send3(d, c).wait_send()

            @pl.when(has[1] if d == FWD else has[0])
            def _():
                sendc(d, c).wait_send()


def local(
    mesh_shape, ssm_input, gate_z, b_proj, c_proj, step_size, log_decay, skip_d, norm_gain, w_out, d_out, game_lengths
):
    n_seq, n_chan, n_dp = (mesh_shape[a] for a in ("seq", "chan", "dp"))
    _, rows, width = ssm_input.shape
    heads = step_size.shape[2]
    states = b_proj.shape[2]
    model = w_out.shape[1]
    nb = d_out.shape[2]
    half = width // 2
    chunks = max(1, min(4, half // 128))
    cw = half // chunks
    reds = 0
    for n in (n_seq, n_dp):
        while n > 1:
            reds += 1
            n //= 2
    peers = max(1, n_chan - 1)
    sizes = (n_seq, n_chan, n_dp, heads, game_lengths.shape[1], chunks)
    vmem = pl.BlockSpec(memory_space=pltpu.VMEM)
    hbm = pl.BlockSpec(memory_space=pl.ANY)
    dma = pltpu.SemaphoreType.DMA
    out, gx, gg, gs = pl.pallas_call(
        functools.partial(kernel, sizes),
        out_shape=(
            jax.ShapeDtypeStruct((rows, nb), BF16),
            jax.ShapeDtypeStruct((rows, width), BF16),
            jax.ShapeDtypeStruct((1, width), F32),
            jax.ShapeDtypeStruct((1, heads), F32),
        ),
        in_specs=[vmem] * 7 + [pl.BlockSpec(memory_space=pltpu.SMEM)] + [hbm] * 3,
        out_specs=(vmem,) * 4,
        scratch_shapes=[
            pltpu.VMEM((rows, width), BF16),
            pltpu.VMEM((width, model), BF16),
            pltpu.VMEM((n_chan, rows, nb), BF16),
            pltpu.VMEM((rows, heads), F32),
            pltpu.VMEM((heads, rows), F32),
            pltpu.VMEM((1, width), F32),
            pltpu.VMEM((1, width), F32),
            pltpu.VMEM((rows, width), F32),
            pltpu.VMEM((rows, width), F32),
            pltpu.VMEM((heads // 2, 2 * rows, rows), BF16),
            pltpu.VMEM((rows, width), F32),
            pltpu.VMEM((rows, width), F32),
            pltpu.VMEM((rows, width), F32),
            pltpu.VMEM((rows, width), BF16),
            pltpu.VMEM((rows, width), F32),
            pltpu.VMEM((rows, width), BF16),
            pltpu.VMEM((chunks, states, cw), F32),
            pltpu.VMEM((2, chunks, states, cw), BF16),
            pltpu.VMEM((2, chunks, states, cw), BF16),
            pltpu.VMEM((2, chunks, states, cw), BF16),
            pltpu.VMEM((2, chunks, states, cw), BF16),
            pltpu.VMEM((2, chunks, states, cw), BF16),
            pltpu.VMEM((2, 2 * chunks, states, cw), BF16),
            pltpu.VMEM((8, rows), F32),
            pltpu.VMEM((peers, 8, rows), F32),
            pltpu.VMEM((peers, rows, nb), BF16),
            pltpu.VMEM((peers, rows, nb), BF16),
            pltpu.VMEM((reds + 1, 2, width), F32),
            pltpu.VMEM((reds, 2, width), F32),
            dma((2,)),
            dma,
            dma((peers,)),
            dma((peers,)),
            dma((2,)),
            dma((2, chunks)),
            dma((2, chunks)),
            dma((2, chunks)),
            dma((2, chunks)),
            dma((2, chunks)),
            dma((2, chunks)),
            dma((peers,)),
            dma((peers,)),
            dma((peers,)),
            dma((peers,)),
            dma((reds,)),
            dma((reds,)),
        ],
        compiler_params=pltpu.CompilerParams(
            collective_id=0, has_side_effects=True, vmem_limit_bytes=60 * 1024 * 1024
        ),
    )(
        ssm_input[0],
        b_proj[0],
        c_proj[0],
        step_size[0],
        log_decay[0],
        skip_d[None],
        norm_gain[None],
        game_lengths,
        gate_z[0],
        w_out,
        d_out[0],
    )
    return out[None], gx[None], gg[0], gs[0]


def solution(mesh):
    return jax.shard_map(
        functools.partial(local, dict(mesh.shape)),
        mesh=mesh,
        in_specs=(
            P("dp", "seq", "chan"),
            P("dp", "seq", "chan"),
            P("dp", "seq", None),
            P("dp", "seq", None),
            P("dp", "seq", "chan"),
            P("dp", "seq", "chan"),
            P("chan"),
            P("chan"),
            P("chan", None),
            P("dp", "seq", "chan"),
            P("dp", None),
        ),
        out_specs=(P("dp", "seq", "chan"), P("dp", "seq", "chan"), P("chan"), P("chan")),
        check_vma=False,
    )
```

time: 249 us -> 68.5 us (0.28)
  the two profiles are of different devices: /device:TPU:0 before, /device:TPU:25 now
where the time goes in v1:
time: 68.5 us; the launch traced here: 68.1 us
  Pallas kernels  58.6 us (86%)
  local copies, waits for them, and re-layouts  8.87 us (13%)
    pallas_call x1, Pallas kernels, local(): pl.pallas_call(functools.partial(kernel, sizes), out_shape=(jax.ShapeDtyp...  58.6 us
    unnamed x6, local copies, waits for them, and re-layouts  8.87 us

profile of v1, /device:TPU:25, one launch (start us, length us, event | category | flops | bytes accessed | tf_op | source)
XLA Modules:
  0.0 68.1 jit_solution(16845160527023252998)
XLA Ops:
  0.6 1.4 %copy.15 = f32[1,128,32]{2,1,0:T(8,128)} copy(f32[1,128,32]{1,2,0:T(8,128)} %param.15) | data formatting | bytes 32768 | tf_op args[4]
  2.1 1.4 %copy.16 = f32[1,128,32]{2,1,0:T(8,128)} copy(f32[1,128,32]{1,2,0:T(8,128)} %param.16) | data formatting | bytes 32768 | tf_op args[5]
  3.5 58.6 %shard_map.138 = (bf16[128,1024]{1,0:T(8,128)(2,1)}, bf16[128,2048]{1,0:T(8,128)(2,1)}, f32[1,2048]{1,0:T(1,128)}, f32[1,32]{1,0:T(1,128)}) custom-call(bf16[128,2048]{1,0:T(8,128)(2,1)} %bitcast.13, bf16[128,128]{1,0:T(8,128)(2,1)} %bitcast.20, bf16[128,128]{1,0:T(8,128)(2,1)} %bitcast.21, f32[128,32]{1,0:T(8,128)} %bitcast.16, f32[128,32]{1,0:T(8,128)} %bitcast.17, ...), custom_call_target="tpu_custom_call" | custom-call | tf_op jit(solution)/shard_map/pallas_call | solution.py:492
  62.1 1.7 %copy.21 = bf16[1,128,1024]{2,1,0:T(8,128)(2,1)} copy(bf16[1,128,1024]{2,1,0:T(8,128)(2,1)} %bitcast.19) | data formatting | bytes 524288
  63.8 1.9 %copy.22 = bf16[1,128,2048]{2,1,0:T(8,128)(2,1)} copy(bf16[1,128,2048]{2,1,0:T(8,128)(2,1)} %bitcast.15) | data formatting | bytes 1048576
  65.7 1.3 %copy.23 = f32[2048]{0:T(1024)} copy(f32[2048]{0:T(1024)} %bitcast.22) | data formatting | bytes 16384
  67.0 1.1 %copy.24 = f32[32]{0:T(128)} copy(f32[32]{0:T(128)} %bitcast.25) | data formatting | bytes 256

commit v2 on v1

--- a/solution.py
+++ b/solution.py
@@ -79,6 +79,7 @@
     stat_rx,
     proj_tx,
     proj_rx,
+    proj_own,
     red_tx,
     red_rx,
     load_sem,
@@ -116,18 +117,13 @@
 
     steps = []
     hop = 1
-    while hop < n_seq:
-        steps.append({"seq": seq + hop - 2 * hop * lax.rem(seq // hop, 2)})
-        hop *= 2
-    hop = 1
     while hop < n_dp:
         steps.append({"dp": dp + hop - 2 * hop * lax.rem(dp // hop, 2)})
         hop *= 2
+    steps.append(partner)
+    far = [{"seq": lax.rem(seq + 2 * k, n_seq)} for k in range(1, n_seq // 2)]
     chan_peers = [{"chan": lax.rem(chan + off, n_chan)} for off in range(1, n_chan)]
-    greet = steps + chan_peers + [
-        {"seq": lax.rem(seq + 2, n_seq)},
-        {"seq": lax.rem(seq + n_seq - 2, n_seq)},
-    ]
+    greet = steps + chan_peers + far
     barrier = pltpu.get_barrier_semaphore()
     for peer in greet:
         pl.semaphore_signal(barrier, inc=1, device_id=peer, device_id_type=MESH)
@@ -152,7 +148,7 @@
     tri = causal.astype(F32).astype(BF16)
     running = jnp.zeros((rows, heads), F32)
     for part in split(ld_ref[...], 3):
-        running = running + dot(tri, part)
+        running = running + dot_cols(tri, part)
     running_ref[...] = running
     run_row[...] = running.T
     base = seq * rows
@@ -185,14 +181,18 @@
             total = piece if total is None else total + piece
         return total
 
-    tdt_e[...] = expand(tail * dt_ref[...], 2)
+    tdt_e[...] = expand(tail * dt_ref[...].T, 2)
     row_pad = jnp.concatenate([decay, skip_ref[...], jnp.zeros((6, heads), F32)], axis=0)
     rows_e = expand(row_pad, 3)
     decay_row[...] = rows_e[0:1, :]
     skip_e = rows_e[1:2, :]
 
-    def other_cols(c):
-        return pl.ds(pl.multiple_of((1 - mine) * half + c * cw, cw), cw)
+    group = 2 if chunks % 2 == 0 else 1
+    groups = chunks // group
+    gw = group * cw
+
+    def half_cols(which, g):
+        return pl.ds(pl.multiple_of(which * half + g * gw, gw), gw)
 
     def my_cols(c):
         return pl.ds(pl.multiple_of(mine * half + c * cw, cw), cw)
@@ -213,17 +213,21 @@
     dec = remote(decay_row, decay_peer, dec_sem.at[0], dec_sem.at[1], partner)
 
     def make(d, left, value_of):
-        for c in range(chunks):
-            tx1[d, c] = dot(left, value_of(other_cols(c))).astype(BF16)
-            send1(d, c).start()
-        for c in range(chunks):
-            own_ref[c] = dot(left, value_of(my_cols(c)))
+        for g in range(groups):
+            block = dot(left, value_of(half_cols(1 - mine, g))).astype(BF16)
+            for k in range(group):
+                tx1[d, g * group + k] = block[:, k * cw : (k + 1) * cw]
+                send1(d, g * group + k).start()
+        for g in range(groups):
+            block = dot(left, value_of(half_cols(mine, g)))
+            for k in range(group):
+                own_ref[g * group + k] = block[:, k * cw : (k + 1) * cw]
 
     def chain(d):
         first = mine == (0 if d == FWD else 1)
         prev, nxt = (has[0], has[1]) if d == FWD else (has[1], has[0])
 
-        def body(c, _):
+        def body(c):
             send1(d, c).wait_recv()
 
             @pl.when(prev)
@@ -250,24 +254,32 @@
                 sendc(d, c).start()
 
             tx3[d, c] = jnp.where(first, after_me, before).astype(BF16)
-            send3(d, c).start()
+
+            @pl.when(prev)
+            def _():
+                send3(d, c).start()
+
             state_ref[d, mine * chunks + c] = jnp.where(first, before, after_peer).astype(BF16)
-            return 0
-
-        lax.fori_loop(0, chunks, body, 0)
+
+        for c in range(chunks):
+            body(c)
+
+        @pl.when(jnp.logical_not(prev))
+        def _():
+            for c in range(chunks):
+                send3(d, c).start()
 
     pl.semaphore_wait(barrier, len(greet))
     dec.start()
-    b_t = b_ref[...].T
-    make(FWD, b_t, lambda cols: (tdt_e[:, cols] * x_ref[:, cols].astype(F32)).astype(BF16))
     loads[2].wait()
     do_copies = []
     for k, peer in enumerate(chan_peers):
         do_copies.append(remote(dfull.at[0], dfull.at[k + 1], do_send.at[k], do_recv.at[k], peer))
         do_copies[-1].start()
+    b_t = b_ref[...].T
+    make(FWD, b_t, lambda cols: (tdt_e[:, cols] * x_ref[:, cols].astype(F32)).astype(BF16))
 
     scores = jnp.where(causal & (count_col == count_row), dot_cols(c_ref[...], b_ref[...]), 0.0)
-    dt_row = dt_ref[...].T
     pos_lane = lax.broadcasted_iota(jnp.int32, (rows, 2 * hd), 1) < hd
     carry_e[...] = expand(carry, 2)
     loads[0].wait()
@@ -283,7 +295,7 @@
         mixes = []
         for h in (2 * q, 2 * q + 1):
             gap = jnp.minimum(running_ref[:, h : h + 1] - run_row[h : h + 1, :], 0.0)
-            mixes.append((jnp.exp(gap) * scores * dt_row[h : h + 1, :]).astype(BF16))
+            mixes.append((jnp.exp(gap) * scores * dt_ref[h : h + 1, :]).astype(BF16))
             mix_ref[q, (h % 2) * rows : (h % 2 + 1) * rows, :] = mixes[-1]
         pair = x_ref[:, cols]
         inside_ref[:, cols] = dot(jnp.concatenate(mixes, axis=1), block_diag(pair)) + skip_e[
@@ -292,52 +304,59 @@
         zf = z_ref[:, cols].astype(F32)
         act_ref[:, cols] = zf / (1.0 + jnp.exp(-zf))
 
+    tile = min(256, width)
+
+    def pull():
+        loads[1].wait()
+        for copy in do_copies:
+            copy.wait_recv()
+
+        def body(i, _):
+            feats = pl.ds(pl.multiple_of(i * tile, tile), tile)
+            total = None
+            for k in range(n_chan):
+                source = lax.rem(chan + n_chan - k, n_chan)
+                piece = dot_cols(dfull[k], w_ref[feats, pl.ds(pl.multiple_of(source * nb, nb), nb)])
+                total = piece if total is None else total + piece
+            pulled_ref[:, feats] = total
+            return 0
+
+        lax.fori_loop(0, width // tile, body, 0)
+
+    pl.when(place == last)(pull)
     dec.wait_recv()
     chain(FWD)
-
-    loads[1].wait()
-    for copy in do_copies:
-        copy.wait_recv()
-    tile = min(256, width)
-
-    def pull(i, _):
-        feats = pl.ds(pl.multiple_of(i * tile, tile), tile)
-        total = None
-        for k in range(n_chan):
-            source = lax.rem(chan + n_chan - k, n_chan)
-            piece = dot_cols(dfull[k], w_ref[feats, pl.ds(pl.multiple_of(source * nb, nb), nb)])
-            total = piece if total is None else total + piece
-        pulled_ref[:, feats] = total
-        return 0
-
-    lax.fori_loop(0, width // tile, pull, 0)
+    pl.when(place < last)(pull)
 
     def gate(q, sums):
         squares, dots = sums
-        cols = pl.ds(pl.multiple_of(q * cw, cw), cw)
-        carried = dot(c_ref[...], state_ref[FWD, q])
+        cols = pl.ds(pl.multiple_of(q * gw, gw), gw)
+        carried = jnp.concatenate(
+            [dot(c_ref[...], state_ref[FWD, q * group + k]) for k in range(group)], axis=1
+        )
         gated = (inside_ref[:, cols] + carry_e[:, cols] * carried) * act_ref[:, cols]
         normed = (gated * gain_ref[:, cols]).astype(BF16)
         gated_ref[:, cols] = gated
         normed_ref[:, cols] = normed
         sq = gated * gated
         od = normed.astype(F32) * pulled_ref[:, cols]
-        for k in range(cw // 128):
+        for k in range(gw // 128):
             squares = squares + sq[:, k * 128 : (k + 1) * 128]
             dots = dots + od[:, k * 128 : (k + 1) * 128]
         return squares, dots
 
     zero = jnp.zeros((rows, 128), F32)
-    sums = lax.fori_loop(0, chunks, lambda c, s: gate(mine * chunks + c, s), (zero, zero))
+    sums = lax.fori_loop(0, groups, lambda g, s: gate(mine * groups + g, s), (zero, zero))
 
     def gate_late(d):
-        def body(c, s):
-            send3(d, c).wait_recv()
-            return gate((1 - mine) * chunks + c, s)
+        def body(g, s):
+            for k in range(group):
+                send3(d, g * group + k).wait_recv()
+            return gate((1 - mine) * groups + g, s)
 
         return body
 
-    squares, dots = lax.fori_loop(0, chunks, gate_late(FWD), sums)
+    squares, dots = lax.fori_loop(0, groups, gate_late(FWD), sums)
     sq_col = jnp.sum(squares, axis=1, keepdims=True)
     dot_col = jnp.sum(dots, axis=1, keepdims=True)
     lane = lax.broadcasted_iota(jnp.int32, (rows, 128), 1)
@@ -355,21 +374,27 @@
     inv = lax.rsqrt(stat_cols[:, 0:1] / total_width + NORM_EPS)
     back = inv * inv * inv * stat_cols[:, 1:2] / total_width
 
-    def cot(q, _):
-        cols = pl.ds(pl.multiple_of(q * cw, cw), cw)
+    c_t = c_ref[...].T
+
+    def cot_block(cols):
         gated = gated_ref[:, cols]
         d_normed = inv * pulled_ref[:, cols]
         d = ((gain_ref[:, cols] * d_normed - back * gated) * act_ref[:, cols]).astype(BF16)
         d_ref[:, cols] = d
-        red_tx[0, 0:1, cols] = jnp.sum(gated * d_normed, axis=0, keepdims=True)
+        pulled_ref[:, cols] = gated * d_normed
+        return (carry_e[:, cols] * d.astype(F32)).astype(BF16)
+
+    make(BWD, c_t, cot_block)
+
+    def cot(q, _):
+        cols = pl.ds(pl.multiple_of(q * gw, gw), gw)
+        red_tx[0, 0:1, cols] = jnp.sum(pulled_ref[:, cols], axis=0, keepdims=True)
         red_tx[0, 1:2, cols] = jnp.sum(
-            d.astype(F32) * x_ref[:, cols].astype(F32), axis=0, keepdims=True
+            d_ref[:, cols].astype(F32) * x_ref[:, cols].astype(F32), axis=0, keepdims=True
         )
         return 0
 
-    lax.fori_loop(0, 2 * chunks, cot, 0)
-    c_t = c_ref[...].T
-    make(BWD, c_t, lambda cols: (carry_e[:, cols] * d_ref[:, cols].astype(F32)).astype(BF16))
+    lax.fori_loop(0, 2 * groups, cot, 0)
 
     def red(k):
         return remote(red_tx.at[k], red_rx.at[k], rd_send.at[k], rd_recv.at[k], steps[k])
@@ -380,8 +405,11 @@
         if k + 1 < len(steps):
             red(k + 1).start()
 
+    def red_far(k):
+        slot = len(steps) + k
+        return remote(red_tx.at[len(steps)], red_rx.at[slot], rd_send.at[slot], rd_recv.at[slot], far[k])
+
     red(0).start()
-
     tile_n = min(256, nb)
 
     def project(block, store):
@@ -402,49 +430,64 @@
         pj_copies.append(remote(proj_tx.at[k], proj_rx.at[k], pj_send.at[k], pj_recv.at[k], peer))
         pj_copies[-1].start()
 
-    chain(BWD)
+    pl.when(place == last)(lambda: chain(BWD))
     reduce_step(0)
-
-    own_tiles = []
-    for i in range(nb // tile_n):
+    def own_body(i, _):
         at = pl.ds(pl.multiple_of(chan * nb + i * tile_n, tile_n), tile_n)
-        own_tiles.append(dot(normed_ref[...], w_ref[:, at]))
-    for copy in pj_copies:
-        copy.wait_recv()
-    for i in range(nb // tile_n):
-        at = slice(i * tile_n, (i + 1) * tile_n)
-        value = own_tiles[i]
-        for k in range(n_chan - 1):
-            value = value + proj_rx[k, :, at].astype(F32)
-        out_ref[:, at] = (inv * value).astype(BF16)
-    if len(steps) > 1:
-        reduce_step(1)
-
+        proj_own[:, pl.ds(pl.multiple_of(i * tile_n, tile_n), tile_n)] = dot(normed_ref[...], w_ref[:, at])
+        return 0
+
+    lax.fori_loop(0, nb // tile_n, own_body, 0)
     for q in range(heads // 2):
         cols = slice(q * 2 * hd, (q + 1) * 2 * hd)
         pair = d_ref[:, cols]
         inside_ref[:, cols] = dot_rows(mix_ref[q], block_diag(pair)) + skip_e[:, cols] * pair.astype(F32)
-    for k in range(2, len(steps)):
-        reduce_step(k)
+
+    def finish_out():
+        for copy in pj_copies:
+            copy.wait_recv()
+        for i in range(nb // tile_n):
+            at = slice(i * tile_n, (i + 1) * tile_n)
+            value = proj_own[:, at]
+            for k in range(n_chan - 1):
+                value = value + proj_rx[k, :, at].astype(F32)
+            out_ref[:, at] = (inv * value).astype(BF16)
+
+    def settle():
+        for k in range(1, len(steps)):
+            reduce_step(k)
+        for k in range(len(far)):
+            red_far(k).start()
+        finish_out()
+
+    pl.when(place < last - 1)(settle)
+    pl.when(place < last)(lambda: chain(BWD))
+    pl.when(place >= last - 1)(settle)
 
     def finish(q):
-        cols = pl.ds(pl.multiple_of(q * cw, cw), cw)
-        carried = dot(b_ref[...], state_ref[BWD, q])
+        cols = pl.ds(pl.multiple_of(q * gw, gw), gw)
+        carried = jnp.concatenate(
+            [dot(b_ref[...], state_ref[BWD, q * group + k]) for k in range(group)], axis=1
+        )
         gx_ref[:, cols] = (inside_ref[:, cols] + tdt_e[:, cols] * carried).astype(BF16)
 
-    def early(c, _):
-        finish(mine * chunks + c)
+    def early(g, _):
+        finish(mine * groups + g)
         return 0
 
-    def late(c, _):
-        send3(BWD, c).wait_recv()
-        finish((1 - mine) * chunks + c)
+    def late(g, _):
+        for k in range(group):
+            send3(BWD, g * group + k).wait_recv()
+        finish((1 - mine) * groups + g)
         return 0
 
-    lax.fori_loop(0, chunks, early, 0)
-    lax.fori_loop(0, chunks, late, 0)
+    lax.fori_loop(0, groups, early, 0)
+    lax.fori_loop(0, groups, late, 0)
 
     final = red_tx[len(steps)]
+    for k in range(len(far)):
+        red_far(k).wait_recv()
+        final = final + red_rx[len(steps) + k]
     gg_ref[...] = final[0:1, :]
     skip_cols = jnp.concatenate([final[1:2, :], jnp.zeros((7, width), F32)], axis=0)
     skip_sum = jnp.zeros((8, heads), F32)
@@ -457,6 +500,8 @@
         copy.wait_send()
     for k in range(len(steps)):
         red(k).wait_send()
+    for k in range(len(far)):
+        red_far(k).wait_send()
     for d in (FWD, BWD):
         for c in range(chunks):
             send1(d, c).wait_send()
@@ -465,6 +510,11 @@
             @pl.when(has[1] if d == FWD else has[0])
             def _():
                 sendc(d, c).wait_send()
+
+
+def hand_over(*refs):
+    for source, target in zip(refs[:4], refs[4:]):
+        target[...] = source[...]
 
 
 def local(
@@ -477,17 +527,14 @@
     model = w_out.shape[1]
     nb = d_out.shape[2]
     half = width // 2
-    chunks = max(1, min(4, half // 128))
+    chunks = max(1, min(8, half // 128))
     cw = half // chunks
-    reds = 0
-    for n in (n_seq, n_dp):
-        while n > 1:
-            reds += 1
-            n //= 2
+    reds = n_dp.bit_length()
+    slots = reds + n_seq // 2 - 1
     peers = max(1, n_chan - 1)
     sizes = (n_seq, n_chan, n_dp, heads, game_lengths.shape[1], chunks)
     vmem = pl.BlockSpec(memory_space=pltpu.VMEM)
-    hbm = pl.BlockSpec(memory_space=pl.ANY)
+    hbm = pl.BlockSpec(memory_space=pltpu.HBM)
     dma = pltpu.SemaphoreType.DMA
     out, gx, gg, gs = pl.pallas_call(
         functools.partial(kernel, sizes),
@@ -527,8 +574,9 @@
             pltpu.VMEM((peers, 8, rows), F32),
             pltpu.VMEM((peers, rows, nb), BF16),
             pltpu.VMEM((peers, rows, nb), BF16),
+            pltpu.VMEM((rows, nb), F32),
             pltpu.VMEM((reds + 1, 2, width), F32),
-            pltpu.VMEM((reds, 2, width), F32),
+            pltpu.VMEM((slots, 2, width), F32),
             dma((2,)),
             dma,
             dma((peers,)),
@@ -544,8 +592,8 @@
             dma((peers,)),
             dma((peers,)),
             dma((peers,)),
-            dma((reds,)),
-            dma((reds,)),
+            dma((slots,)),
+            dma((slots,)),
         ],
         compiler_params=pltpu.CompilerParams(
             collective_id=0, has_side_effects=True, vmem_limit_bytes=60 * 1024 * 1024
@@ -554,8 +602,8 @@
         ssm_input[0],
         b_proj[0],
         c_proj[0],
-        step_size[0],
-        log_decay[0],
+        step_size[0].T,
+        log_decay[0].T,
         skip_d[None],
         norm_gain[None],
         game_lengths,
@@ -563,6 +611,13 @@
         w_out,
         d_out[0],
     )
+    results = (out, gx, gg, gs)
+    out, gx, gg, gs = pl.pallas_call(
+        hand_over,
+        out_shape=tuple(jax.ShapeDtypeStruct(a.shape, a.dtype) for a in results),
+        in_specs=[vmem] * 4,
+        out_specs=(vmem,) * 4,
+    )(*results)
     return out[None], gx[None], gg[0], gs[0]
 
 

time: 68.5 us -> 54.1 us (0.79)
  the two profiles are of different devices: /device:TPU:25 before, /device:TPU:0 now
where the time goes in v2:
time: 54.1 us; the launch traced here: 53.9 us
  Pallas kernels  53.3 us (99%)
  between operations  0.64 us (1%)
    pallas_call x1, Pallas kernels, local(): pl.pallas_call(functools.partial(kernel, sizes), out_shape=(jax.ShapeDtyp...  51.3 us
    pallas_call x1, Pallas kernels, local(): pl.pallas_call(hand_over, out_shape=tuple((jax.ShapeDtypeStruct(a.shape,...  2.03 us

profile of v2, /device:TPU:0, one launch (start us, length us, event | category | flops | bytes accessed | tf_op | source)
XLA Modules:
  0.0 53.9 jit_solution(6986562640236905679)
XLA Ops:
  0.6 51.3 %shard_map.138 = (bf16[128,1024]{1,0:T(8,128)(2,1)}, bf16[128,2048]{1,0:T(8,128)(2,1)}, f32[1,2048]{1,0:T(1,128)}, f32[1,32]{1,0:T(1,128)}) custom-call(bf16[128,2048]{1,0:T(8,128)(2,1)} %bitcast.17, bf16[128,128]{1,0:T(8,128)(2,1)} %bitcast.20, bf16[128,128]{1,0:T(8,128)(2,1)} %bitcast.21, f32[32,128]{1,0:T(8,128)} %bitcast.22, f32[32,128]{1,0:T(8,128)} %bitcast.23, ...), custom_call_target="tpu_custom_call" | custom-call | tf_op jit(solution)/shard_map/pallas_call | solution.py:539
  51.9 2.0 %shard_map.139 = (bf16[128,1024]{1,0:T(8,128)(2,1)}, bf16[128,2048]{1,0:T(8,128)(2,1)}, f32[1,2048]{1,0:T(1,128)}, f32[1,32]{1,0:T(1,128)}) custom-call(bf16[128,1024]{1,0:T(8,128)(2,1)} %get-tuple-element.12.refs_0_, bf16[128,2048]{1,0:T(8,128)(2,1)} %get-tuple-element.13.refs_1_, f32[1,2048]{1,0:T(1,128)} %get-tuple-element.14.refs_2_, ...), custom_call_target="tpu_custom_call" | custom-call | tf_op jit(solution)/shard_map/pallas_call | solution.py:615

commit v3 on v2

--- a/solution.py
+++ b/solution.py
@@ -264,10 +264,9 @@
         for c in range(chunks):
             body(c)
 
-        @pl.when(jnp.logical_not(prev))
-        def _():
-            for c in range(chunks):
-                send3(d, c).start()
+    def head_sends(d):
+        for c in range(chunks):
+            send3(d, c).start()
 
     pl.semaphore_wait(barrier, len(greet))
     dec.start()
@@ -326,6 +325,7 @@
     pl.when(place == last)(pull)
     dec.wait_recv()
     chain(FWD)
+    pl.when(place == 0)(lambda: head_sends(FWD))
     pl.when(place < last)(pull)
 
     def gate(q, sums):
@@ -463,6 +463,7 @@
     pl.when(place < last - 1)(settle)
     pl.when(place < last)(lambda: chain(BWD))
     pl.when(place >= last - 1)(settle)
+    pl.when(place == last)(lambda: head_sends(BWD))
 
     def finish(q):
         cols = pl.ds(pl.multiple_of(q * gw, gw), gw)
@@ -539,10 +540,10 @@
     out, gx, gg, gs = pl.pallas_call(
         functools.partial(kernel, sizes),
         out_shape=(
-            jax.ShapeDtypeStruct((rows, nb), BF16),
-            jax.ShapeDtypeStruct((rows, width), BF16),
-            jax.ShapeDtypeStruct((1, width), F32),
-            jax.ShapeDtypeStruct((1, heads), F32),
+            pltpu.VMEM((rows, nb), BF16),
+            pltpu.VMEM((rows, width), BF16),
+            pltpu.VMEM((1, width), F32),
+            pltpu.VMEM((1, heads), F32),
         ),
         in_specs=[vmem] * 7 + [pl.BlockSpec(memory_space=pltpu.SMEM)] + [hbm] * 3,
         out_specs=(vmem,) * 4,
@@ -617,6 +618,7 @@
         out_shape=tuple(jax.ShapeDtypeStruct(a.shape, a.dtype) for a in results),
         in_specs=[vmem] * 4,
         out_specs=(vmem,) * 4,
+        compiler_params=pltpu.CompilerParams(vmem_limit_bytes=4 * 1024 * 1024),
     )(*results)
     return out[None], gx[None], gg[0], gs[0]
 

time: 54.1 us -> 50.6 us (0.935)
  Pallas kernels: 53.3 us -> 49.8 us
    pallas_call x1, Pallas kernels: 51.3 us -> 48.9 us  [local(): pl.pallas_call(functools.partial(kernel, sizes), out_shape=(pltpu.VMEM((r...]
    pallas_call x1, Pallas kernels: 2.03 us -> 0.93 us  [local(): pl.pallas_call(hand_over, out_shape=tuple((jax.ShapeDtypeStruct(a.shape,...]
where the time goes in v3:
time: 50.6 us; the launch traced here: 50.5 us
  Pallas kernels  49.8 us (98%)
  between operations  0.64 us (1%)
    pallas_call x1, Pallas kernels, local(): pl.pallas_call(functools.partial(kernel, sizes), out_shape=(pltpu.VMEM((r...  48.9 us

profile of v3, /device:TPU:0, one launch (start us, length us, event | category | flops | bytes accessed | tf_op | source)
XLA Modules:
  0.0 50.5 jit_solution(4425249286192740878)
XLA Ops:
  0.6 48.9 %shard_map.138 = (bf16[128,1024]{1,0:T(8,128)(2,1)S(1)}, bf16[128,2048]{1,0:T(8,128)(2,1)S(1)}, f32[1,2048]{1,0:T(1,128)S(1)}, f32[1,32]{1,0:T(1,128)S(1)}) custom-call(bf16[128,2048]{1,0:T(8,128)(2,1)} %bitcast.17, bf16[128,128]{1,0:T(8,128)(2,1)} %bitcast.20, bf16[128,128]{1,0:T(8,128)(2,1)} %bitcast.21, f32[32,128]{1,0:T(8,128)} %bitcast.22, ...), custom_call_target="tpu_custom_call" | custom-call | tf_op jit(solution)/shard_map/pallas_call | solution.py:540
  49.5 0.9 %shard_map.139 = (bf16[128,1024]{1,0:T(8,128)(2,1)}, bf16[128,2048]{1,0:T(8,128)(2,1)}, f32[1,2048]{1,0:T(1,128)}, f32[1,32]{1,0:T(1,128)}) custom-call(bf16[128,1024]{1,0:T(8,128)(2,1)S(1)} %get-tuple-element.12.refs_0_, bf16[128,2048]{1,0:T(8,128)(2,1)S(1)} %get-tuple-element.13.refs_1_, f32[1,2048]{1,0:T(1,128)S(1)} %get-tuple-element.14.refs_2_, ...), custom_call_target="tpu_custom_call" | custom-call | tf_op jit(solution)/shard_map/pallas_call | solution.py:616

commit v4 on v3

--- a/solution.py
+++ b/solution.py
@@ -37,7 +37,7 @@
 
 def kernel(
     sizes,
-    x_ref,
+    x_hbm,
     b_ref,
     c_ref,
     dt_ref,
@@ -52,6 +52,7 @@
     gx_ref,
     gg_ref,
     gs_ref,
+    x_ref,
     z_ref,
     w_ref,
     dfull,
@@ -133,6 +134,8 @@
         pltpu.make_async_copy(w_hbm, w_ref, load_sem.at[1]),
         pltpu.make_async_copy(do_hbm, dfull.at[0], dl_sem),
     ]
+    load_x = pltpu.make_async_copy(x_hbm, x_ref, load_sem.at[2])
+    load_x.start()
     loads[2].start()
     loads[0].start()
     loads[1].start()
@@ -268,6 +271,7 @@
         for c in range(chunks):
             send3(d, c).start()
 
+    load_x.wait()
     pl.semaphore_wait(barrier, len(greet))
     dec.start()
     loads[2].wait()
@@ -545,9 +549,10 @@
             pltpu.VMEM((1, width), F32),
             pltpu.VMEM((1, heads), F32),
         ),
-        in_specs=[vmem] * 7 + [pl.BlockSpec(memory_space=pltpu.SMEM)] + [hbm] * 3,
+        in_specs=[hbm] + [vmem] * 6 + [pl.BlockSpec(memory_space=pltpu.SMEM)] + [hbm] * 3,
         out_specs=(vmem,) * 4,
         scratch_shapes=[
+            pltpu.VMEM((rows, width), BF16),
             pltpu.VMEM((rows, width), BF16),
             pltpu.VMEM((width, model), BF16),
             pltpu.VMEM((n_chan, rows, nb), BF16),
@@ -578,7 +583,7 @@
             pltpu.VMEM((rows, nb), F32),
             pltpu.VMEM((reds + 1, 2, width), F32),
             pltpu.VMEM((slots, 2, width), F32),
-            dma((2,)),
+            dma((3,)),
             dma,
             dma((peers,)),
             dma((peers,)),

time: 50.6 us -> 50.8 us (level)
  no operation moved by 1% of the time
where the time goes in v4:
time: 50.8 us; the launch traced here: 50.6 us
  Pallas kernels  49.9 us (98%)
  between operations  0.64 us (1%)
    pallas_call x1, Pallas kernels, local(): pl.pallas_call(functools.partial(kernel, sizes), out_shape=(pltpu.VMEM((r...  49 us

profile of v4, /device:TPU:0, one launch (start us, length us, event | category | flops | bytes accessed | tf_op | source)
XLA Modules:
  0.0 50.6 jit_solution(11886480745728592820)
XLA Ops:
  0.6 49.0 %shard_map.138 = (bf16[128,1024]{1,0:T(8,128)(2,1)S(1)}, bf16[128,2048]{1,0:T(8,128)(2,1)S(1)}, f32[1,2048]{1,0:T(1,128)S(1)}, f32[1,32]{1,0:T(1,128)S(1)}) custom-call(bf16[128,2048]{1,0:T(8,128)(2,1)} %bitcast.17, bf16[128,128]{1,0:T(8,128)(2,1)} %bitcast.20, bf16[128,128]{1,0:T(8,128)(2,1)} %bitcast.21, f32[32,128]{1,0:T(8,128)} %bitcast.22, ...), custom_call_target="tpu_custom_call" | custom-call | tf_op jit(solution)/shard_map/pallas_call | solution.py:544
  49.7 0.9 %shard_map.139 = (bf16[128,1024]{1,0:T(8,128)(2,1)}, bf16[128,2048]{1,0:T(8,128)(2,1)}, f32[1,2048]{1,0:T(1,128)}, f32[1,32]{1,0:T(1,128)}) custom-call(bf16[128,1024]{1,0:T(8,128)(2,1)S(1)} %get-tuple-element.12.refs_0_, bf16[128,2048]{1,0:T(8,128)(2,1)S(1)} %get-tuple-element.13.refs_1_, f32[1,2048]{1,0:T(1,128)S(1)} %get-tuple-element.14.refs_2_, ...), custom_call_target="tpu_custom_call" | custom-call | tf_op jit(solution)/shard_map/pallas_call | solution.py:621
